TPU v7x, 512 devices: a whole 4x4x16 slice. The times are simulated.
512 devices in a mesh: param: 128 (over z, y, core), sensor: 4 (over x).
Axes of the slice: x: 4, y: 4, z: 16, core: 2. Of those that a mesh axis runs over, the one named last changes fastest.
Arguments:
- blocks: bfloat16 [64, 2, 600, 16384], P(None, None, 'sensor', 'param'), may hold values from -0.1875 to 0.1875
- probes: bfloat16 [64, 2, 4, 16384], P(None, None, None, 'param'), may hold values from -6 to 6
Outputs:
- basis: float32 [64, 2, 4, 600], P(None, None, None, 'sensor')
- coeffs: bfloat16 [64, 2, 4, 16384], P('sensor', None, None, 'param')
All inputs are finite; a program needn't handle non-finite values.
Results may differ from a plain program's by a relative error of at most 0.0049.
Values sent between devices are 32-bit elements; how exact they have to be, the bound alone decides.
A program may use at most 64 MiB of HBM per device.

v0:
```python
import jax
import jax.numpy as jnp
from jax import lax
from jax.sharding import Mesh
from jax.sharding import PartitionSpec as P

SENSORS = 600
FREQ_LINES = 64
PARAM = ("param_0", "param_1", "param_2")


def split_up(x, dim, length):
    before, after = (x.shape[:dim], x.shape[dim + 1 :])
    return jnp.moveaxis(x.reshape(*before, length, -1, *after), dim, 0)


def sent_and_summed(x, axis, dim):
    length = lax.axis_size(axis)
    pieces = lax.all_to_all(split_up(x, dim, length), axis, 0, 0, tiled=True)
    return jnp.sum(pieces, axis=0)


def sum_by_axis(x, axes, dim):
    far, near = axes
    pieces = split_up(x, dim, lax.axis_size(far))
    nearer = sent_and_summed(pieces, near, dim + 1)
    arrived = lax.all_to_all(nearer, far, split_axis=0, concat_axis=0, tiled=True)
    return arrived.sum(axis=0)


def filled_up(lines, length):
    spare = -len(lines) % length
    return jnp.pad(lines, [(0, spare)] + [(0, 0)] * (lines.ndim - 1))


def from_everyone(x, axis):
    copies = jnp.broadcast_to(x, (lax.axis_size(axis), *x.shape))
    return lax.all_to_all(copies, axis, split_axis=0, concat_axis=0, tiled=True)


def in_order(pieces, dim):
    pieces = jnp.moveaxis(pieces, 0, dim)
    dims = pieces.shape
    return pieces.reshape(*dims[:dim], dims[dim] * dims[dim + 1], *dims[dim + 2 :])


def gathered_by_axis(x, axes, dim):
    far, near = axes
    initial = from_everyone(x, far)
    pieces = jnp.swapaxes(from_everyone(initial, near), 0, 1)
    return in_order(pieces.reshape(-1, *x.shape), dim)


def nested_sum(x, axes):
    lines = x.reshape(-1, x.shape[-1])
    own = sum_by_axis(filled_up(lines, lax.axis_size(axes[0]) * lax.axis_size(axes[1])), axes, 0)
    whole = gathered_by_axis(own, axes, 0)
    return whole[: len(lines)].reshape(x.shape)


def over_copies(x, axis):
    everything = from_everyone(x, axis)
    return jnp.sum(everything, axis=0)


def local_gram(values):
    return jnp.einsum("fas,fbs->ab", values, values, precision=lax.Precision.HIGHEST) / (
        2.0 * FREQ_LINES * SENSORS
    )


def inverse_factor(gram):
    lower = jnp.linalg.cholesky(gram)
    return lax.linalg.triangular_solve(
        lower, jnp.eye(gram.shape[0], dtype=gram.dtype), left_side=True, lower=True
    )


def on_device(blocks, probes):
    block_real = blocks[:, 0]
    block_imag = blocks[:, 1]
    probe_real = probes[:, 0]
    probe_imag = probes[:, 1]
    lines = blocks.shape[0]
    group = blocks.shape[2]
    count = probes.shape[2]
    real_part = jnp.einsum(
        "fsn,fan->fas", block_real, probe_real, preferred_element_type=jnp.float32
    ) - jnp.einsum("fsn,fan->fas", block_imag, probe_imag, preferred_element_type=jnp.float32)
    imag_part = jnp.einsum(
        "fsn,fan->fas", block_real, probe_imag, preferred_element_type=jnp.float32
    ) + jnp.einsum("fsn,fan->fas", block_imag, probe_real, preferred_element_type=jnp.float32)
    partial_sketch = jnp.stack([real_part, imag_part], axis=1).reshape(2 * lines, count, group)
    sketch = nested_sum(partial_sketch, (("param_0", "param_1"), "param_2"))
    gram = over_copies(local_gram(sketch), "sensor")
    inverse = inverse_factor(gram)
    flat_basis = jnp.einsum("ab,fbs->fas", inverse, sketch, precision=lax.Precision.HIGHEST)
    basis = flat_basis.reshape(lines, 2, count, group)
    rounded = basis.astype(jnp.bfloat16)
    vector_real = rounded[:, 0]
    vector_imag = rounded[:, 1]
    adjoint_real = jnp.einsum(
        "fsn,fas->fan", block_real, vector_real, preferred_element_type=jnp.float32
    ) + jnp.einsum("fsn,fas->fan", block_imag, vector_imag, preferred_element_type=jnp.float32)
    adjoint_imag = jnp.einsum(
        "fsn,fas->fan", block_real, vector_imag, preferred_element_type=jnp.float32
    ) - jnp.einsum("fsn,fas->fan", block_imag, vector_real, preferred_element_type=jnp.float32)
    terms = jnp.stack([adjoint_real, adjoint_imag], axis=1)
    coeffs = sent_and_summed(terms, "sensor", 0).astype(jnp.bfloat16)
    return (basis, coeffs)


def solution(mesh):
    torus = Mesh(
        mesh.devices.reshape(16, 4, 2, mesh.shape["sensor"]),
        ("param_0", "param_1", "param_2", "sensor"),
    )
    placed = (P(None, None, "sensor", PARAM), P(None, None, None, PARAM))
    return jax.shard_map(
        on_device,
        mesh=torus,
        in_specs=placed,
        out_specs=(P(None, None, None, "sensor"), P("sensor", None, None, PARAM)),
        check_vma=False,
    )
```

profile of v0, /device:TPU:1, one launch (start us, length us, event | category | flops | bytes accessed | tf_op | source)
XLA Modules:
  0.0 123.5 jit_solution(599551092945345436)
XLA Ops:
  0.6 10.0 %fusion.20 = (bf16[64,1,150,128]{3,1,2,0:T(2,128)(2,1)S(1)}, bf16[64,1,150,128]{3,1,2,0:T(2,128)(2,1)S(1)}) fusion(bf16[64,2,150,128]{3,1,2,0:T(2,128)(2,1)} %param.2), kind=kLoop, calls=%fused_computation.40 | loop fusion | bytes 9830400 | tf_op jit(solution)/shard_map/slice | solution.py:81
  10.7 0.7 copy_bitcast_fusion
  11.3 0.2 copy-done.3
  11.5 1.4 %fusion.6 = f32[64,4,150]{2,1,0:T(4,128)S(1)} fusion(bf16[64,150,128]{2,1,0:T(8,128)(2,1)S(1)} %get-tuple-element.13, bf16[64,2,4,128]{3,2,1,0:T(4,128)(2,1)S(1)} %copy-done.3), kind=kOutput, calls=%fused_computation.20 | convolution fusion | flops 9830400 | bytes 2709504 | tf_op jit(solution)/shard_map/fsn,fan->fas/dot_general | solution.py:90
  12.9 1.4 %fusion.10 = f32[64,4,150]{2,1,0:T(4,128)S(1)} fusion(bf16[64,150,128]{2,1,0:T(8,128)(2,1)S(1)} %get-tuple-element.13, bf16[64,2,4,128]{3,2,1,0:T(4,128)(2,1)S(1)} %copy-done.3), kind=kOutput, calls=%fused_computation.24 | convolution fusion | flops 9830400 | bytes 2709504 | tf_op jit(solution)/shard_map/fsn,fan->fas/dot_general | solution.py:87
  14.3 1.4 %fusion = f32[64,1,4,150]{3,2,0,1:T(4,128)S(1)} fusion(f32[64,4,150]{2,1,0:T(4,128)S(1)} %fusion.6, bf16[64,150,128]{2,1,0:T(8,128)(2,1)S(1)} %get-tuple-element.12, bf16[64,2,4,128]{3,2,1,0:T(4,128)(2,1)S(1)} %copy-done.3), kind=kOutput, calls=%fused_computation.4 | convolution fusion | flops 9868800 | bytes 2971648 | tf_op jit(solution)/shard_map/fsn,fan->fas/dot_general | solution.py:92
  15.7 1.4 %fusion.1 = f32[64,1,4,150]{3,2,0,1:T(4,128)S(1)} fusion(f32[64,4,150]{2,1,0:T(4,128)S(1)} %fusion.10, bf16[64,150,128]{2,1,0:T(8,128)(2,1)S(1)} %get-tuple-element.12, bf16[64,2,4,128]{3,2,1,0:T(4,128)(2,1)S(1)} %copy-done.3), kind=kOutput, calls=%fused_computation.6 | convolution fusion | flops 9868800 | bytes 2971648 | tf_op jit(solution)/shard_map/fsn,fan->fas/dot_general | solution.py:89
  17.1 0.1 maximum_bitcast_fusion
  17.3 10.6 %all_to_all.30 = f32[2,64,4,150]{3,2,1,0:T(4,128)S(1)} all-to-all(f32[2,64,4,150]{3,2,1,0:T(4,128)S(1)} %maximum_bitcast_fusion), channel_id=1, replica_groups=mesh['param_0'=16,'param_1'=4,'param_2'=2,'sensor'=4] {'param_2'}, dimensions={0} | all-to-all | bytes 614400 | tf_op jit(solution)/shard_map/all_to_all | solution.py:19
  27.9 0.2 reduce_sum.36
  28.1 33.1 %all_to_all.31 = f32[64,4,150]{2,1,0:T(4,128)S(1)} all-to-all(f32[64,4,150]{2,1,0:T(4,128)S(1)} %reduce_sum.36), channel_id=1, replica_groups=mesh['param_0'=16,'param_1'=4,'param_2'=2,'sensor'=4] {'param_0','param_1'}, dimensions={0} | all-to-all | bytes 307200 | tf_op jit(solution)/shard_map/all_to_all | solution.py:27
  61.3 25.3 %all_to_all.32 = f32[64,4,150]{2,1,0:T(4,128)S(1)} all-to-all(f32[64,4,150]{2,1,0:T(4,128)S(1)} %broadcast_in_dim.9), channel_id=1, replica_groups=mesh['param_0'=16,'param_1'=4,'param_2'=2,'sensor'=4] {'param_0','param_1'}, dimensions={0} | all-to-all | bytes 307200 | tf_op jit(solution)/shard_map/all_to_all | solution.py:38
  86.7 8.5 %all_to_all.33 = f32[2,64,4,150]{3,2,1,0:T(4,128)S(1)} all-to-all(f32[2,64,4,150]{3,2,1,0:T(4,128)S(1)} %broadcast_in_dim.10), channel_id=1, replica_groups=mesh['param_0'=16,'param_1'=4,'param_2'=2,'sensor'=4] {'param_2'}, dimensions={0} | all-to-all | bytes 614400 | tf_op jit(solution)/shard_map/all_to_all | solution.py:38
  95.2 2.3 %fusion.2 = f32[4,4]{1,0:T(4,128)S(1)} fusion(f32[2,64,4,150]{3,2,1,0:T(4,128)S(1)} %all_to_all.33), kind=kOutput, calls=%fused_computation.11 | convolution fusion | flops 3686416 | bytes 307264 | tf_op jit(solution)/shard_map/fas,fbs->ab/dot_general | solution.py:67
  97.5 0.6 broadcast_in_dim.11
  98.1 4.0 %all-to-all-start.4 = ((f32[4,4,4]{2,1,0:T(4,128)}), f32[4,4,4]{2,1,0:T(4,128)S(1)}, u32[]{:S(2)}, u32[]{:S(2)}) async-start(f32[4,4,4]{2,1,0:T(4,128)} %broadcast_in_dim.11), calls=%async_computation.4 | async-start | bytes 16384 | tf_op jit(solution)/shard_map/all_to_all | solution.py:38
  102.2 0.3 copy.58
  102.4 3.9 %all-to-all-done.4 = f32[4,4,4]{2,1,0:T(4,128)S(1)} async-done(((f32[4,4,4]{2,1,0:T(4,128)}), f32[4,4,4]{2,1,0:T(4,128)S(1)}, u32[]{:S(2)}, u32[]{:S(2)}) %all-to-all-start.4) | async-done | bytes 288 | tf_op jit(solution)/shard_map/all_to_all | solution.py:38
  106.3 0.1 copy.56
  106.4 0.4 cholesky.17
  106.8 0.6 compare_reduce_fusion
  107.5 0.6 fusion.16
  108.1 0.3 custom-call.6
  108.5 0.2 convolution_bitcast_fusion.1
  108.7 0.7 convolution_bitcast_fusion
  109.3 0.3 copy.59
  109.7 2.7 %fusion.5 = f32[64,4,128]{2,1,0:T(4,128)S(1)} fusion(bf16[64,150,128]{2,1,0:T(8,128)(2,1)} %copy-done, bf16[64,2,4,150]{3,2,0,1:T(4,128)(2,1)S(1)} %copy.79), kind=kOutput, calls=%fused_computation.19 | convolution fusion | flops 9830400 | bytes 2719744 | tf_op jit(solution)/shard_map/fsn,fas->fan/dot_general | solution.py:105
  112.4 0.8 fusion.4
  113.2 0.8 convolution_add_fusion.1
  114.0 0.8 convolution_subtract_fusion.1
  114.9 7.9 %all_to_all.34 = f32[4,16,2,4,128]{4,3,1,2,0:T(4,128)S(1)} all-to-all(f32[4,16,2,4,128]{4,3,1,2,0:T(4,128)S(1)} %pad_maximum_fusion), channel_id=1, replica_groups=mesh['param_0'=16,'param_1'=4,'param_2'=2,'sensor'=4] {'sensor'}, dimensions={0} | all-to-all | bytes 524288 | tf_op jit(solution)/shard_map/all_to_all | solution.py:19
  122.8 0.6 copy.64
  (17 shorter events, 0.5 us)
Async XLA Ops:
  10.6 0.9 copy-start.3
  11.3 3.0 %copy-start = (bf16[64,150,128]{2,1,0:T(8,128)(2,1)}, bf16[64,150,128]{2,1,0:T(8,128)(2,1)S(1)}, u32[]{:S(2)}) copy-start(bf16[64,150,128]{2,1,0:T(8,128)(2,1)S(1)} %get-tuple-element.13) | copy-start | bytes 7372804
  98.1 8.2 %all-to-all-start.4 = ((f32[4,4,4]{2,1,0:T(4,128)}), f32[4,4,4]{2,1,0:T(4,128)S(1)}, u32[]{:S(2)}, u32[]{:S(2)}) async-start(f32[4,4,4]{2,1,0:T(4,128)} %broadcast_in_dim.11), calls=%async_computation.4 | async-start | bytes 16384 | tf_op jit(solution)/shard_map/all_to_all | solution.py:38
  109.6 3.6 %copy-start.2 = (f32[128,4,150]{2,1,0:T(4,128)}, f32[128,4,150]{2,1,0:T(4,128)S(1)}, u32[]{:S(2)}) copy-start(f32[128,4,150]{2,1,0:T(4,128)S(1)} %copy.59) | copy-start | bytes 921604
  109.6 2.8 %copy-start.1 = (bf16[64,150,128]{2,1,0:T(8,128)(2,1)S(1)}, bf16[64,150,128]{2,1,0:T(8,128)(2,1)}, u32[]{:S(2)}) copy-start(bf16[64,150,128]{2,1,0:T(8,128)(2,1)} %copy-done) | copy-start | bytes 7372804
where the time goes:
time: 125 us; the launch traced here: 123 us
  blocking collectives  85.4 us (68%)
  matrix products  13.8 us (11%)
  local copies, waits for them, and re-layouts  13 us (10%)
  starting transfers between devices  4.01 us (3%)
  waiting for transfers between devices  3.87 us (3%)
  other arithmetic  2.6 us (2%)
    all_to_all x2, blocking collectives, from_everyone(): return lax.all_to_all(copies, axis, split_axis=0, concat_axis=0, tiled=True)  33.8 us
    all_to_all x1, blocking collectives, sum_by_axis(): lax.all_to_all(nearer, far, split_axis=0, concat_axis=0, tiled=True)  33.1 us
    all_to_all x2, blocking collectives, sent_and_summed(): pieces = lax.all_to_all(split_up(x, dim, length), axis, 0, 0, tiled=True)  18.5 us
    slice x1, local copies, waits for them, and re-layouts, on_device(): block_imag = blocks[:, 1]  10 us
    all_to_all x1, starting transfers between devices, from_everyone(): return lax.all_to_all(copies, axis, split_axis=0, concat_axis=0, tiled=True)  4.01 us
    all_to_all x1, waiting for transfers between devices, from_everyone(): return lax.all_to_all(copies, axis, split_axis=0, concat_axis=0, tiled=True)  3.87 us
    dot_general x1, matrix products, on_device(): jnp.einsum('fsn,fas->fan', block_real, vector_imag, preferred_element_typ...  2.72 us
  transfers between devices with their start and end apart: 1, of which 1 were waited for; matrix products, arithmetic and copies ran while one was open for 0% of the time, Pallas kernels for 0%

commit v1 on v0

v1 whole, which is shorter than its diff:
```python
import functools

import jax
import jax.numpy as jnp
from jax import lax
from jax.experimental import pallas as pl
from jax.experimental.pallas import tpu as pltpu
from jax.sharding import Mesh
from jax.sharding import PartitionSpec as P

SENSORS = 600
FREQ_LINES = 64
PARAM = ("param_0", "param_1", "param_2")
Z, Y, C, X = 16, 4, 2, 4
MESH = pl.DeviceIdType.MESH
MAIN = 8
TILES = 10
GROUPS = 8
GROUP = 150
TAIL = GROUP - 128
F32 = jnp.float32
BF16 = jnp.bfloat16


def owner_of(tile, c):
    return jnp.where(tile < MAIN, 2 * tile + c, 5 + 8 * (tile - MAIN) - c)


def cholesky_inverse(g):
    low = [[None] * 4 for _ in range(4)]
    inv = [[None] * 4 for _ in range(4)]
    for a in range(4):
        for b in range(a + 1):
            rest = g[a][b]
            for k in range(b):
                rest = rest - low[a][k] * low[b][k]
            low[a][b] = jnp.sqrt(rest) if a == b else rest / low[b][b]
    for b in range(4):
        inv[b][b] = 1.0 / low[b][b]
        for a in range(b + 1, 4):
            total = low[a][b] * inv[b][b]
            for k in range(b + 1, a):
                total = total + low[a][k] * inv[k][b]
            inv[a][b] = -total / low[a][a]
    return inv


def kernel(
    blocks_hbm, probes_hbm, basis_hbm, coef_hbm,
    blk, prb, tmp, part, from_core, ysum, from_y, zsum, from_z, full, gram_in, gram_out, gram_core,
    basis, terms, from_x, coef,
    load_sem, probe_sem, core_send, core_recv, ys_send, ys_recv, zs_send, zs_recv,
    za_send, za_recv, ya_send, ya_recv, ca_send, ca_recv, gx_send, gx_recv, gc_send, gc_recv,
    xs_send, xs_recv, out_sem,
):
    z, y, c, x = (lax.axis_index(n) for n in ("param_0", "param_1", "param_2", "sensor"))
    at = lambda z_, y_, c_, x_: (z_, y_, c_, x_)
    sibling = at(z, y, 1 - c, x)

    pltpu.make_async_copy(probes_hbm, prb, probe_sem).start()

    def load(k):
        g = lax.rem((1 - c) * 4 + k, GROUPS)
        return pltpu.make_async_copy(
            blocks_hbm.at[pl.ds(g * MAIN, MAIN)], blk.at[pl.ds(g * MAIN, MAIN)], load_sem.at[k]
        )

    for k in range(GROUPS):
        load(k).start()
    barrier = pltpu.get_barrier_semaphore()
    for d in range(1, Z):
        pl.semaphore_signal(barrier, inc=1, device_id=at(lax.rem(z + d, Z), y, c, x), device_id_type=MESH)
    for e in range(1, X * Y):
        pl.semaphore_signal(
            barrier, inc=1,
            device_id=at(z, lax.rem(y + e % Y, Y), c, lax.rem(x + e // Y, X)),
            device_id_type=MESH,
        )
    pl.semaphore_signal(barrier, inc=1, device_id=sibling, device_id_type=MESH)

    row = lax.broadcasted_iota(jnp.int32, (8, 128), 0)
    lane = lax.broadcasted_iota(jnp.int32, (8, 128), 1)
    plus = jnp.where(row < 4, -1.0, 1.0).astype(F32)
    tmp[...] = jnp.zeros_like(tmp)
    pltpu.make_async_copy(probes_hbm, prb, probe_sem).wait()

    def sketch_group(k, carry):
        load(k).wait()
        g = lax.rem((1 - c) * 4 + k, GROUPS)
        for q in range(2):
            tails = jnp.zeros((8, 128), F32)
            for j in range(4):
                i = 4 * q + j
                f = g * MAIN + i
                probe = prb[f]
                turned = (plus * pltpu.roll(probe.astype(F32), 4, 0)).astype(BF16)
                left = jnp.concatenate([probe, turned], axis=1)
                right = jnp.concatenate([blk[f, 0], blk[f, 1]], axis=1)
                value = lax.dot_general(
                    left, right, (((1,), (1,)), ((), ())), preferred_element_type=F32
                )
                part[g, i] = value[:, :128]
                tmp[i, :, :GROUP] = value
                tail = tmp[i, :, 128:]
                tails = tails + (tail if j == 0 else pltpu.roll(tail, 32 * j, 1))
            part[g, MAIN + q] = tails
        return carry

    lax.fori_loop(0, GROUPS, sketch_group, 0)
    pl.semaphore_wait(barrier, Z - 1 + X * Y - 1 + 1)

    def to_core(d):
        yy = lax.rem(y + d, Y)
        return pltpu.make_async_remote_copy(
            src_ref=part.at[(1 - c) * 4 + yy], dst_ref=from_core.at[d],
            send_sem=core_send.at[d], recv_sem=core_recv.at[d],
            device_id=sibling, device_id_type=MESH,
        )

    def to_y(d):
        return pltpu.make_async_remote_copy(
            src_ref=ysum.at[d], dst_ref=from_y.at[d],
            send_sem=ys_send.at[d], recv_sem=ys_recv.at[d],
            device_id=at(z, lax.rem(y + d, Y), c, x), device_id_type=MESH,
        )

    for d in (2, 1, 3, 0):
        to_core(d).start()
    for d in (2, 1, 3, 0):
        to_core(d).wait_recv()
        ysum[d] = part[c * 4 + lax.rem(y + d, Y)] + from_core[d]
        if d:
            to_y(d).start()
    for d in (1, 3, 2):
        to_y(d).wait_recv()
    zsum[...] = (ysum[0] + from_y[1]) + (from_y[2] + from_y[3])

    def to_owner(i):
        o = owner_of(i, c)
        d = lax.rem(o - z + Z, Z)
        return d, pltpu.make_async_remote_copy(
            src_ref=zsum.at[i], dst_ref=from_z.at[d],
            send_sem=zs_send.at[i], recv_sem=zs_recv.at[d],
            device_id=at(o, y, c, x), device_id_type=MESH,
        )

    for k in range(TILES):
        d, copy = to_owner(k)

        @pl.when(d != 0)
        def _():
            copy.start()

    is_main = lax.rem(z + c, 2) == 0
    is_tail = lax.rem(z + c, 8) == 5
    mine = jnp.where(is_main, (z - c) // 2, MAIN + (z + c - 5) // 8)
    owns = jnp.logical_or(is_main, is_tail)
    group = c * 4 + y

    def to_ring(d):
        return pltpu.make_async_remote_copy(
            src_ref=full.at[group, mine], dst_ref=full.at[group, mine],
            send_sem=za_send.at[d], recv_sem=za_recv.at[mine],
            device_id=at(lax.rem(z + d, Z), y, c, x), device_id_type=MESH,
        )

    order = [8, 7, 9, 6, 10, 5, 11, 4, 12, 3, 13, 2, 14, 1, 15]

    @pl.when(owns)
    def _():
        total = zsum[mine]
        for d in reversed(order):
            pltpu.make_async_remote_copy(
                src_ref=zsum.at[0], dst_ref=from_z.at[d],
                send_sem=zs_send.at[0], recv_sem=zs_recv.at[d],
                device_id=sibling, device_id_type=MESH,
            ).wait_recv()
            total = total + from_z[d]
        full[group, mine] = total
        for d in order:
            to_ring(d).start()

    for i in range(TILES):
        d, _ = to_owner(i)

        @pl.when(d != 0)
        def _():
            pltpu.make_async_remote_copy(
                src_ref=full.at[group, i], dst_ref=full.at[group, i],
                send_sem=za_send.at[0], recv_sem=za_recv.at[i],
                device_id=sibling, device_id_type=MESH,
            ).wait_recv()

    def to_y_all(d):
        return pltpu.make_async_remote_copy(
            src_ref=full.at[group], dst_ref=full.at[group],
            send_sem=ya_send.at[d], recv_sem=ya_recv.at[d],
            device_id=at(z, lax.rem(y + d, Y), c, x), device_id_type=MESH,
        )

    def to_core_all(d, who):
        g = who * 4 + lax.rem(y - d + Y, Y)
        return pltpu.make_async_remote_copy(
            src_ref=full.at[g], dst_ref=full.at[g],
            send_sem=ca_send.at[d], recv_sem=ca_recv.at[d],
            device_id=sibling, device_id_type=MESH,
        )

    for d in (2, 1, 3):
        to_y_all(d).start()
    to_core_all(0, c).start()

    sums = []
    own = [full[group, i] for i in range(TILES)]
    for k in range(4):
        acc = None
        for tile in own:
            prod = tile * (tile if k == 0 else pltpu.roll(tile, k, 0))
            acc = prod if acc is None else acc + prod
        sums.append(jnp.sum(acc, axis=1, keepdims=True))
    packed = jnp.zeros((8, 128), F32)
    for k in range(4):
        packed = jnp.where(lane == k, sums[k], packed)
    gram_out[...] = packed

    def gram_to(e):
        return pltpu.make_async_remote_copy(
            src_ref=gram_out, dst_ref=gram_in.at[e],
            send_sem=gx_send.at[e], recv_sem=gx_recv.at[e],
            device_id=at(z, lax.rem(y + e % Y, Y), c, lax.rem(x + e // Y, X)), device_id_type=MESH,
        )

    for e in range(1, X * Y):
        gram_to(e).start()
    for d in (1, 3, 2):
        pltpu.make_async_remote_copy(
            src_ref=full.at[group], dst_ref=full.at[c * 4 + lax.rem(y - d + Y, Y)],
            send_sem=ya_send.at[d], recv_sem=ya_recv.at[d],
            device_id=sibling, device_id_type=MESH,
        ).wait_recv()
        to_core_all(d, c).start()
    total = packed
    for e in range(1, X * Y):
        gram_to(e).wait_recv()
        total = total + gram_in[e]
    gram_core[0] = total
    to_gram_core = pltpu.make_async_remote_copy(
        src_ref=gram_core.at[0], dst_ref=gram_core.at[1],
        send_sem=gc_send, recv_sem=gc_recv, device_id=sibling, device_id_type=MESH,
    )
    to_gram_core.start()
    to_gram_core.wait_recv()
    total = total + gram_core[1]
    total = (total + pltpu.roll(total, 4, 0)) / (2.0 * FREQ_LINES * SENSORS)
    g = [[None] * 4 for _ in range(4)]
    for a in range(4):
        for b in range(a + 1):
            picked = jnp.where(jnp.logical_and(row == a, lane == a - b), total, 0.0)
            g[a][b] = jnp.sum(jnp.sum(picked, axis=1, keepdims=True), axis=0, keepdims=True)
    inv = cholesky_inverse(g)
    probe_of = lax.rem(row, 4)
    mix = []
    for k in range(4):
        column = jnp.zeros((8, 128), F32)
        for a in range(k, 4):
            column = jnp.where(probe_of == a, jnp.broadcast_to(inv[a][a - k], (8, 128)), column)
        mix.append(column)

    def mixed(tile):
        out = mix[0] * tile
        for k in range(1, 4):
            out = out + mix[k] * pltpu.roll(tile, k, 0)
        return out

    for d in range(4):
        to_core_all(d, 1 - c).wait_recv()

    minus = -plus

    def to_x(d):
        return pltpu.make_async_remote_copy(
            src_ref=terms.at[d], dst_ref=from_x.at[d],
            send_sem=xs_send.at[d], recv_sem=xs_recv.at[d],
            device_id=at(z, y, c, lax.rem(x + d, X)), device_id_type=MESH,
        )

    for d in (2, 1, 3, 0):
        first = lax.rem(x + d, X) * (FREQ_LINES // X)

        def adjoint_quad(q, carry, d=d, first=first):
            f0 = first + q * 4
            g = f0 // MAIN
            half = lax.rem(q, 2)
            tails = mixed(full[g, MAIN + half])
            for j in range(4):
                f = f0 + j
                main = mixed(full[g, half * 4 + j])
                tail = tails if j == 0 else pltpu.roll(tails, 128 - 32 * j, 1)
                value = jnp.concatenate([main, tail], axis=1)[:, :GROUP]
                basis[f, 0] = value[:4]
                basis[f, 1] = value[4:]
                right = jnp.concatenate([blk[f, 0], blk[f, 1]], axis=1)
                both = jnp.dot(value.astype(BF16), right, preferred_element_type=F32)
                terms[d, q * 4 + j] = both[:, :128] + minus * pltpu.roll(both[:, 128:], 4, 0)
            return carry

        lax.fori_loop(0, FREQ_LINES // X // 4, adjoint_quad, 0)
        if d:
            to_x(d).start()
    basis_out = pltpu.make_async_copy(basis, basis_hbm, out_sem.at[0])
    basis_out.start()
    for d in (1, 3, 2):
        to_x(d).wait_recv()

    def add_up(i, carry):
        coef[i] = ((terms[0, i] + from_x[1, i]) + (from_x[2, i] + from_x[3, i])).astype(BF16)
        return carry

    lax.fori_loop(0, FREQ_LINES // X, add_up, 0)
    coef_out = pltpu.make_async_copy(coef, coef_hbm, out_sem.at[1])
    coef_out.start()

    for d in range(4):
        to_core(d).wait_send()
        to_core_all(d, c).wait_send()
    for d in range(1, 4):
        to_y(d).wait_send()
        to_y_all(d).wait_send()
        to_x(d).wait_send()
    for i in range(TILES):
        d, copy = to_owner(i)

        @pl.when(d != 0)
        def _():
            copy.wait_send()

    @pl.when(owns)
    def _():
        for d in order:
            to_ring(d).wait_send()

    for e in range(1, X * Y):
        gram_to(e).wait_send()
    to_gram_core.wait_send()
    basis_out.wait()
    coef_out.wait()


def on_device(blocks, probes):
    tile = (8, 128)
    dma = pltpu.SemaphoreType.DMA
    basis, coef = pl.pallas_call(
        kernel,
        out_shape=(
            jax.ShapeDtypeStruct((FREQ_LINES, 2, 4, GROUP), F32),
            jax.ShapeDtypeStruct((FREQ_LINES // X, 8, 128), BF16),
        ),
        in_specs=[pl.BlockSpec(memory_space=pl.ANY)] * 2,
        out_specs=(pl.BlockSpec(memory_space=pl.ANY),) * 2,
        scratch_shapes=[
            pltpu.VMEM((FREQ_LINES, 2, GROUP, 128), BF16),
            pltpu.VMEM((FREQ_LINES, 8, 128), BF16),
            pltpu.VMEM((MAIN, 8, 256), F32),
            pltpu.VMEM((GROUPS, TILES, *tile), F32),
            pltpu.VMEM((4, TILES, *tile), F32),
            pltpu.VMEM((4, TILES, *tile), F32),
            pltpu.VMEM((4, TILES, *tile), F32),
            pltpu.VMEM((TILES, *tile), F32),
            pltpu.VMEM((Z, *tile), F32),
            pltpu.VMEM((GROUPS, TILES, *tile), F32),
            pltpu.VMEM((X * Y, *tile), F32),
            pltpu.VMEM(tile, F32),
            pltpu.VMEM((2, *tile), F32),
            pltpu.VMEM((FREQ_LINES, 2, 4, GROUP), F32),
            pltpu.VMEM((X, FREQ_LINES // X, *tile), F32),
            pltpu.VMEM((X, FREQ_LINES // X, *tile), F32),
            pltpu.VMEM((FREQ_LINES // X, *tile), BF16),
            dma((GROUPS,)), dma,
            dma((4,)), dma((4,)),
            dma((4,)), dma((4,)),
            dma((TILES,)), dma((Z,)),
            dma((Z,)), dma((TILES,)),
            dma((4,)), dma((4,)),
            dma((4,)), dma((4,)),
            dma((X * Y,)), dma((X * Y,)),
            dma, dma,
            dma((4,)), dma((4,)),
            dma((2,)),
        ],
        compiler_params=pltpu.CompilerParams(
            collective_id=0, has_side_effects=True, vmem_limit_bytes=48 * 1024 * 1024
        ),
    )(blocks, probes.reshape(FREQ_LINES, 8, 128))
    return basis, coef.reshape(FREQ_LINES // X, 2, 4, 128)


def solution(mesh):
    torus = Mesh(
        mesh.devices.reshape(Z, Y, C, mesh.shape["sensor"]),
        ("param_0", "param_1", "param_2", "sensor"),
    )
    placed = (P(None, None, "sensor", PARAM), P(None, None, None, PARAM))
    return jax.shard_map(
        on_device,
        mesh=torus,
        in_specs=placed,
        out_specs=(P(None, None, None, "sensor"), P("sensor", None, None, PARAM)),
        check_vma=False,
    )
```

time: 125 us -> 57.8 us (0.46); the launches traced: 123 us -> 57.7 us
  blocking collectives: 85.4 us -> 0 us
  Pallas kernels: 0 us -> 52.5 us
  matrix products: 13.8 us -> 0 us
  local copies, waits for them, and re-layouts: 13 us -> 4.53 us
  starting transfers between devices: 4.01 us -> 0 us
  waiting for transfers between devices: 3.87 us -> 0 us
  other arithmetic: 2.6 us -> 0 us
    all_to_all x5 -> x0, blocking collectives: 85.4 us -> none  [the longest x2 33.8 us: from_everyone(): return lax.all_to_all(copies, axis, split_axis=0, concat_axis=0, tiled=True)]
    pallas_call x0 -> x1, Pallas kernels: none -> 52.5 us  [on_device(): pl.pallas_call(kernel, out_shape=(jax.ShapeDtypeStruct((FREQ_LINES, 2, 4,...]
    dot_general x10 -> x0, matrix products: 13.6 us -> none  [the longest x1 2.72 us: on_device(): jnp.einsum('fsn,fas->fan', block_real, vector_imag, preferred_element_typ...]
    slice x1 -> x0, local copies, waits for them, and re-layouts: 10 us -> none  [on_device(): block_imag = blocks[:, 1]]
    all_to_all x1 -> x0, starting transfers between devices: 4.01 us -> none  [from_everyone(): return lax.all_to_all(copies, axis, split_axis=0, concat_axis=0, tiled=True)]
    all_to_all x1 -> x0, waiting for transfers between devices: 3.87 us -> none  [from_everyone(): return lax.all_to_all(copies, axis, split_axis=0, concat_axis=0, tiled=True)]
    unnamed x9 -> x5, local copies, waits for them, and re-layouts: 0.87 us -> 4.53 us
    another operation x6 -> x0, other arithmetic: 2.1 us -> none  [the longest x3 1.03 us: inverse_factor(): lower = jnp.linalg.cholesky(gram)]
  transfers between devices with their start and end apart: 1 -> 0, of which waited for: 1 -> 0; matrix products, arithmetic and copies ran while one was open for 0% -> 0% of each run, Pallas kernels for 0% -> 0%
where the time goes in v1:
time: 57.8 us; the launch traced here: 57.7 us
  Pallas kernels  52.5 us (91%)
  local copies, waits for them, and re-layouts  4.53 us (8%)
  between operations  0.66 us (1%)
    pallas_call x1, Pallas kernels, on_device(): pl.pallas_call(kernel, out_shape=(jax.ShapeDtypeStruct((FREQ_LINES, 2, 4,...  52.5 us
    unnamed x5, local copies, waits for them, and re-layouts  4.53 us

profile of v1, /device:TPU:1, one launch (start us, length us, event | category | flops | bytes accessed | tf_op | source)
XLA Modules:
  0.0 57.7 jit_solution(8196146106463350787)
XLA Ops:
  0.6 0.0 copy-start
  0.6 3.1 %copy.4.blocks_hbm = bf16[64,2,150,128]{3,2,1,0:T(8,128)(2,1)S(1)} copy(bf16[64,2,150,128]{3,1,2,0:T(2,128)(2,1)} %param.2) | data formatting | bytes 9830400 | tf_op args[0]
  3.8 0.0 copy-done
  3.8 52.5 %shard_map.41 = (f32[64,2,4,150]{3,2,1,0:T(4,128)S(1)}, bf16[16,8,128]{2,1,0:T(8,128)(2,1)S(1)}) custom-call(bf16[64,2,150,128]{3,2,1,0:T(8,128)(2,1)S(1)} %copy.4.blocks_hbm, bf16[64,8,128]{2,1,0:T(8,128)(2,1)S(1)} %bitcast.2), custom_call_target="tpu_custom_call" | custom-call | tf_op jit(solution)/shard_map/pallas_call | solution.py:352
  56.3 0.8 %copy.7 = f32[64,2,4,150]{3,2,1,0:T(4,128)} copy(f32[64,2,4,150]{3,2,1,0:T(4,128)S(1)} %get-tuple-element.8) | data formatting | bytes 614400
  57.1 0.6 %copy.8 = bf16[16,2,4,128]{3,2,1,0:T(4,128)(2,1)} copy(bf16[16,2,4,128]{3,2,1,0:T(4,128)(2,1)S(1)} %bitcast.3) | data formatting | bytes 65536
Async XLA Ops:
  0.6 3.1 %copy-start = (bf16[64,2,4,128]{3,2,1,0:T(4,128)(2,1)S(1)}, bf16[64,2,4,128]{3,2,1,0:T(4,128)(2,1)}, u32[]{:S(2)}) copy-start(bf16[64,2,4,128]{3,2,1,0:T(4,128)(2,1)} %param.3) | copy-start | bytes 393220
